TPU v7x, 256 devices: a whole 4x4x8 slice. The times are simulated.
256 devices in a mesh: seq: 64 (over z, y, core), head: 4 (over x).
Axes of the slice: x: 4, y: 4, z: 8, core: 2. Of those that a mesh axis runs over, the one named last changes fastest.
Arguments:
- queries: bfloat16 [16384, 4096], P('seq', 'head'), may hold values from -5 to 5
- keys: bfloat16 [16384, 4096], P('seq', 'head'), may hold values from -5 to 5
- values: bfloat16 [16384, 4096], P('seq', 'head'), may hold values from -6 to 6
- beta: float32 [32], P('head'), may hold values from -2 to 2
- w_out: bfloat16 [4096, 4096], P('head'), may hold values from -0.09375 to 0.09375
Outputs:
- mixed: bfloat16 [16384, 4096], P('seq', 'head')
All inputs are finite; a program needn't handle non-finite values.
Results may differ from a plain program's by a relative error of at most 0.0069.
Values may be sent and summed in bfloat16 or wider, within the bound.
No kernel may reach another device: no remote copies, remote signals or barrier semaphores. Data moves between devices by JAX's collectives and lax.ppermute only.
A program may use at most 192 MiB of HBM per device.

v0:
```python
import jax
import jax.numpy as jnp
from jax import lax
from jax.sharding import Mesh
from jax.sharding import PartitionSpec as P

HD = 128
SEG = 2048
SEQ = ("seq_0", "seq_1", "seq_2")


def passed_along(block, axis, distance):
    devices = range(lax.axis_size(axis))
    route = [(i - distance, i) for i in devices if i - distance in devices]
    return lax.ppermute(block, axis, route)


def filled_with(value, identity):
    return jax.tree.map(
        lambda a, e: jnp.broadcast_to(jnp.asarray(e, a.dtype), a.shape), value, identity
    )


def prefix_by_axis(value, axes, combine, identity):
    before = start = filled_with(value, identity)
    total = value
    for axis in reversed(axes):
        length, position = (lax.axis_size(axis), lax.axis_index(axis))
        pieces = jax.tree.map(lambda part: lax.all_gather(part, axis), total)
        inside, total = (start, start)
        for k in range(length):
            passed = k < position
            total = combine(total, jax.tree.map(lambda part: part[k], pieces))
            inside = jax.tree.map(lambda new, old: jnp.where(passed, new, old), total, inside)
        before = combine(inside, before)
    return before


def cut_along(value, dim, length):
    lengths = value.shape
    pieces = value.reshape(*lengths[:dim], length, lengths[dim] // length, *lengths[dim + 1 :])
    return jnp.moveaxis(pieces, dim, 0)


def summed_on_arrival(value, axis, dim):
    length = lax.axis_size(axis)
    pieces = lax.all_to_all(cut_along(value, dim, length), axis, 0, 0, tiled=True)
    return jnp.sum(pieces.astype(jnp.float32), axis=0)


def elu_plus(inputs):
    return jnp.where(inputs > 0, inputs + 1.0, jnp.exp(jnp.minimum(inputs, 0.0)))


def add_pair(earlier, later):
    return (earlier[0] + later[0], earlier[1] + later[1])


def memory_terms(key_block, value_block, heads_here, row_weight):
    token_rows = key_block.shape[0]
    soft_keys = elu_plus(key_block.astype(jnp.float32)).astype(jnp.bfloat16)
    soft_keys = (soft_keys * row_weight[:, None]).reshape(token_rows, heads_here, HD)
    shaped_values = value_block.reshape(token_rows, heads_here, HD)
    outer = jnp.einsum("thd,the->hde", soft_keys, shaped_values, preferred_element_type=jnp.float32)
    totals = jnp.sum(soft_keys, axis=0, dtype=jnp.float32)
    return (outer, totals)


def body(queries, keys, values, beta, w_out):
    token_rows, width = queries.shape
    heads_here = width // HD
    groups = SEG // token_rows
    seq_rank = lax.axis_index(SEQ)
    place = seq_rank % groups
    stacked = jnp.stack((keys, values))
    earlier_blocks = []
    moving = stacked
    for distance in range(1, groups + 1):
        moving = passed_along(moving, SEQ, 1)
        earlier_blocks.append(moving)
    ordered = earlier_blocks[::-1] + [stacked]
    all_keys = jnp.concatenate([block[0] for block in ordered], axis=0)
    all_values = jnp.concatenate([block[1] for block in ordered], axis=0)
    own_ones = jnp.ones((token_rows,), jnp.bfloat16)
    own_outer, own_totals = memory_terms(keys, values, heads_here, own_ones)
    zero_mem = jnp.zeros((heads_here, HD, HD), jnp.float32)
    zero_norm = jnp.zeros((heads_here, HD), jnp.float32)
    memory, norm_prev = prefix_by_axis(
        (own_outer, own_totals), SEQ, add_pair, (zero_mem, zero_norm)
    )
    earlier_rows = groups * token_rows
    row_distance = groups - jnp.arange(earlier_rows) // token_rows
    inside = ((row_distance <= place) & (row_distance < groups)).astype(jnp.bfloat16)
    outer, totals = memory_terms(
        all_keys[:earlier_rows], all_values[:earlier_rows], heads_here, inside
    )
    memory = memory - outer
    norm_prev = norm_prev - totals
    soft_queries = lax.optimization_barrier(
        elu_plus(queries.astype(jnp.float32)).astype(jnp.bfloat16)
    )
    soft_queries = soft_queries.astype(jnp.float32).reshape(token_rows, heads_here, HD)
    numer = jnp.einsum("thd,hde->the", soft_queries, memory, precision=lax.Precision.HIGHEST)
    denom = 1.0 + jnp.einsum("thd,hd->th", soft_queries, norm_prev, precision=lax.Precision.HIGHEST)
    from_memory = numer / denom[..., None]
    scale = HD ** (-0.5)
    key_offset = jnp.arange((groups + 1) * token_rows) - groups * token_rows
    query_offset = jnp.arange(token_rows)
    visible = (
        (key_offset[None, :] <= query_offset[:, None])
        & (key_offset[None, :] > query_offset[:, None] - SEG)
        & (seq_rank * token_rows + key_offset[None, :] >= 0)
    )
    gates = jax.nn.sigmoid(beta)
    outputs = []
    for head_index in range(heads_here):
        lower = head_index * HD
        query_head = queries[:, lower : lower + HD]
        key_head = all_keys[:, lower : lower + HD]
        value_head = all_values[:, lower : lower + HD]
        scores = (
            lax.dot_general(
                query_head, key_head, (((1,), (1,)), ((), ())), preferred_element_type=jnp.float32
            )
            * scale
        )
        scores = jnp.where(visible, scores, -jnp.inf)
        highest = jnp.max(scores, axis=1, keepdims=True)
        weights = jnp.exp(scores - highest)
        total = jnp.sum(weights, axis=1, keepdims=True)
        local = (
            jnp.dot(weights.astype(jnp.bfloat16), value_head, preferred_element_type=jnp.float32)
            / total
        )
        gate = gates[head_index]
        outputs.append(
            (gate * from_memory[:, head_index] + (1.0 - gate) * local).astype(jnp.bfloat16)
        )
    attended = jnp.concatenate(outputs, axis=1)
    partial_out = jnp.dot(attended, w_out, preferred_element_type=jnp.float32)
    summed = summed_on_arrival(partial_out.astype(jnp.bfloat16), "head", 1)
    return summed.astype(jnp.bfloat16)


def solution(mesh):
    torus = Mesh(
        mesh.devices.reshape(8, 4, 2, mesh.shape["head"]), ("seq_0", "seq_1", "seq_2", "head")
    )
    return jax.shard_map(
        body,
        mesh=torus,
        in_specs=(P(SEQ, "head"), P(SEQ, "head"), P(SEQ, "head"), P("head"), P("head", None)),
        out_specs=P(SEQ, "head"),
        check_vma=False,
    )
```

profile of v0, /device:TPU:64, one launch (start us, length us, event | category | flops | bytes accessed | tf_op | source)
XLA Modules:
  0.0 320.4 jit_solution(12599963364403843043)
XLA Ops:
  9.8 16.3 %collective-permute-done = bf16[2,256,1024]{2,1,0:T(8,128)(2,1)S(1)} collective-permute-done((bf16[2,256,1024]{2,1,0:T(8,128)(2,1)S(1)}, bf16[2,256,1024]{2,1,0:T(8,128)(2,1)S(1)}, u32[]{:S(2)}, u32[]{:S(2)}) %collective-permute-start) | collective-permute-done | bytes 1048608 | tf_op jit(solution)/shard_map/ppermute | solution.py:15
  28.0 16.3 %collective-permute-done.1 = bf16[2,256,1024]{2,1,0:T(8,128)(2,1)S(1)} collective-permute-done((bf16[2,256,1024]{2,1,0:T(8,128)(2,1)S(1)}, bf16[2,256,1024]{2,1,0:T(8,128)(2,1)S(1)}, u32[]{:S(2)}, u32[]{:S(2)}) %collective-permute-start.1) | collective-permute-done | bytes 1048608 | tf_op jit(solution)/shard_map/ppermute | solution.py:15
  49.6 13.0 %collective-permute-done.2 = bf16[2,256,1024]{2,1,0:T(8,128)(2,1)} collective-permute-done((bf16[2,256,1024]{2,1,0:T(8,128)(2,1)S(1)}, bf16[2,256,1024]{2,1,0:T(8,128)(2,1)}, u32[]{:S(2)}, u32[]{:S(2)}) %collective-permute-start.2) | collective-permute-done | bytes 1048608 | tf_op jit(solution)/shard_map/ppermute | solution.py:15
  65.8 15.4 %collective-permute-done.3 = bf16[2,256,1024]{2,1,0:T(8,128)(2,1)} collective-permute-done((bf16[2,256,1024]{2,1,0:T(8,128)(2,1)}, bf16[2,256,1024]{2,1,0:T(8,128)(2,1)}, u32[]{:S(2)}, u32[]{:S(2)}) %collective-permute-start.3) | collective-permute-done | bytes 1048608 | tf_op jit(solution)/shard_map/ppermute | solution.py:15
  83.1 3.4 %all-gather.8.cloned.1.call-done = f32[16,128,128]{2,1,0:T(8,128)} async-done(((f32[8,128,128]{2,1,0:T(8,128)}), f32[16,128,128]{2,1,0:T(8,128)}) %all-gather.8.cloned.1.call-update) | async-done | bytes 1048592 | tf_op jit(solution)/shard_map/all_gather | solution.py:29
  90.5 9.2 %collective-permute-done.4 = bf16[2,256,1024]{2,1,0:T(8,128)(2,1)} collective-permute-done((bf16[2,256,1024]{2,1,0:T(8,128)(2,1)}, bf16[2,256,1024]{2,1,0:T(8,128)(2,1)}, u32[]{:S(2)}, u32[]{:S(2)}) %collective-permute-start.4) | collective-permute-done | bytes 1048608 | tf_op jit(solution)/shard_map/ppermute | solution.py:15
  101.7 18.0 %all_gather.34 = f32[4,8,128]{2,1,0:T(8,128)S(1)} all-gather(f32[1,8,128]{2,1,0:T(8,128)S(1)} %slice_add_fusion.21), channel_id=1, replica_groups=mesh['seq_0'=8,'seq_1'=4,'seq_2'=2,'head'=4] {'seq_1'}, dimensions={0}, use_global_device_ids=true | all-gather | bytes 20480 | tf_op jit(solution)/shard_map/all_gather | solution.py:29
  130.6 33.9 %all_gather.35 = f32[8,8,128]{2,1,0:T(8,128)S(1)} all-gather(f32[1,8,128]{2,1,0:T(8,128)S(1)} %slice_add_fusion.18), channel_id=1, replica_groups=mesh['seq_0'=8,'seq_1'=4,'seq_2'=2,'head'=4] {'seq_0'}, dimensions={0}, use_global_device_ids=true | all-gather | bytes 36864 | tf_op jit(solution)/shard_map/all_gather | solution.py:29
  183.2 6.7 %collective-permute-done.7 = bf16[2,256,1024]{2,1,0:T(8,128)(2,1)} collective-permute-done((bf16[2,256,1024]{2,1,0:T(8,128)(2,1)}, bf16[2,256,1024]{2,1,0:T(8,128)(2,1)}, u32[]{:S(2)}, u32[]{:S(2)}) %collective-permute-start.7) | collective-permute-done | bytes 1048608 | tf_op jit(solution)/shard_map/ppermute | solution.py:15
  205.9 3.2 fusion.255
  210.9 3.0 fusion.256
  215.7 3.0 fusion.257
  220.5 3.0 fusion.258
  225.4 3.0 fusion.259
  230.2 3.0 fusion.260
  235.0 3.0 fusion.261
  238.4 3.3 %fusion.262 = (f32[256]{0:T(256)S(1)}, f32[256,2304]{0,1:T(8,128)S(1)}) fusion(bf16[256,1024]{1,0:T(8,128)(2,1)} %param.5, bf16[2304,1024]{1,0:T(8,128)(2,1)} %copy-done.29, pred[2304]{0:T(1024)(128)(4,1)S(1)} %add_compare_fusion, s32[256]{0:T(256)S(1)} %iota_add_fusion.1, s32[2304]{0:T(1024)S(1)} %iota_add_fusion), kind=kOutput, calls=%fused_computation.303 | convolution fusion | flops 155123456 | bytes 3028224 | tf_op jit(solution)/shard_map/dot_general | solution.py:122
  242.2 2.5 convert_reduce_fusion
  245.0 7.9 %fusion.7 = bf16[2048,8,128]{2,1,0:T(8,128)(2,1)} fusion(bf16[2048,8,128]{2,1,0:T(8,128)(2,1)S(1)} %constant_dynamic-update-slice_fusion, bf16[2048]{0:T(1024)(128)(2,1)S(1)} %fusion.247), kind=kLoop, calls=%fused_computation.23 | loop fusion | flops 14680064 | bytes 8392704 | tf_op jit(solution)/shard_map/mul | solution.py:62
  253.0 8.4 %fusion.46 = f32[8,128,128]{2,1,0:T(8,128)S(1)} fusion(bf16[2048,8,128]{2,1,0:T(8,128)(2,1)} %copy-done.28, bf16[2048,8,128]{2,1,0:T(8,128)(2,1)} %fusion.7, f32[8,8,128,128]{3,2,1,0:T(8,128)} %all-gather.6.cloned.1.call-done, f32[1,8,128,128]{3,2,1,0:T(8,128)S(1)} %copy-done.17, f32[8,128,128]{2,1,0:T(8,128)S(1)} %copy-done.16, ...), kind=kOutput, calls=%fused_computation.79 | convolution fusion | flops 540278784 | bytes 16252942 | tf_op jit(solution)/shard_map/thd,the->hde/dot_general | solution.py:64
  262.0 2.9 fusion.192
  269.8 2.6 fusion.174
  274.6 2.4 fusion.162
  284.0 28.5 %all_to_all.5 = bf16[4,256,1024]{2,1,0:T(8,128)(2,1)S(1)} all-to-all(bf16[4,256,1024]{2,1,0:T(8,128)(2,1)S(1)} %bitcast.238), channel_id=1, replica_groups=mesh['seq_0'=8,'seq_1'=4,'seq_2'=2,'head'=4] {'head'}, dimensions={0} | all-to-all | bytes 4194304 | tf_op jit(solution)/shard_map/all_to_all | solution.py:47
  (174 shorter events, 89.4 us)
Async XLA Ops:
  6.5 58.1 %copy-start = (bf16[256,1024]{1,0:T(8,128)(2,1)S(1)}, bf16[256,1024]{1,0:T(8,128)(2,1)}, u32[]{:S(2)}) copy-start(bf16[256,1024]{1,0:T(8,128)(2,1)} %param.7) | copy-start | bytes 1572868
  6.5 80.0 %all-gather.8.cloned.1.call-start = ((), (), s32[]{:S(2)}) async-start(), calls=%async_computation.2 | async-start | bytes 1572864 | tf_op jit(solution)/shard_map/all_gather | solution.py:29
  6.5 113.1 %copy-start.31 = (f32[8]{0:T(128)S(1)}, f32[8]{0:T(128)}, u32[]{:S(2)}) copy-start(f32[8]{0:T(128)} %param.8) | copy-start | bytes 100
  7.9 18.2 %collective-permute-start = (bf16[2,256,1024]{2,1,0:T(8,128)(2,1)S(1)}, bf16[2,256,1024]{2,1,0:T(8,128)(2,1)S(1)}, u32[]{:S(2)}, u32[]{:S(2)}) collective-permute-start(bf16[2,256,1024]{2,1,0:T(8,128)(2,1)S(1)} %pad_maximum_fusion), channel_id=1, source_target_pairs={{0,4},{4,8},{8,12},{12,16},{16,20},{20,24},{24,28},{28,32},{32,36}... | collective-permute-start | bytes 3145736 | tf_op jit(solution)/shard_map/ppermute | solution.py:15
  26.1 18.2 %collective-permute-start.1 = (bf16[2,256,1024]{2,1,0:T(8,128)(2,1)S(1)}, bf16[2,256,1024]{2,1,0:T(8,128)(2,1)S(1)}, u32[]{:S(2)}, u32[]{:S(2)}) collective-permute-start(bf16[2,256,1024]{2,1,0:T(8,128)(2,1)S(1)} %collective-permute-done), channel_id=1, source_target_pairs={{0,4},{4,8},{8,12},{12,16},{16,20},{20,24},{24,28},{28,32},{32,36}... | collective-permute-start | bytes 3145736 | tf_op jit(solution)/shard_map/ppermute | solution.py:15
  44.3 18.3 %collective-permute-start.2 = (bf16[2,256,1024]{2,1,0:T(8,128)(2,1)S(1)}, bf16[2,256,1024]{2,1,0:T(8,128)(2,1)}, u32[]{:S(2)}, u32[]{:S(2)}) collective-permute-start(bf16[2,256,1024]{2,1,0:T(8,128)(2,1)S(1)} %collective-permute-done.1), channel_id=1, source_target_pairs={{0,4},{4,8},{8,12},{12,16},{16,20},{20,24},{24,28},{28,32},{32,36}... | collective-permute-start | bytes 3145736 | tf_op jit(solution)/shard_map/ppermute | solution.py:15
  62.7 18.5 %collective-permute-start.3 = (bf16[2,256,1024]{2,1,0:T(8,128)(2,1)}, bf16[2,256,1024]{2,1,0:T(8,128)(2,1)}, u32[]{:S(2)}, u32[]{:S(2)}) collective-permute-start(bf16[2,256,1024]{2,1,0:T(8,128)(2,1)} %collective-permute-done.2), channel_id=1, source_target_pairs={{0,4},{4,8},{8,12},{12,16},{16,20},{20,24},{24,28},{28,32},{32,36}... | collective-permute-start | bytes 3145736 | tf_op jit(solution)/shard_map/ppermute | solution.py:15
  65.7 110.7 %all-gather.10.cloned.1.call-start = ((), (), s32[]{:S(2)}) async-start(), calls=%async_computation.3 | async-start | bytes 2621440 | tf_op jit(solution)/shard_map/all_gather | solution.py:29
  81.2 18.5 %collective-permute-start.4 = (bf16[2,256,1024]{2,1,0:T(8,128)(2,1)}, bf16[2,256,1024]{2,1,0:T(8,128)(2,1)}, u32[]{:S(2)}, u32[]{:S(2)}) collective-permute-start(bf16[2,256,1024]{2,1,0:T(8,128)(2,1)} %collective-permute-done.3), channel_id=1, source_target_pairs={{0,4},{4,8},{8,12},{12,16},{16,20},{20,24},{24,28},{28,32},{32,36}... | collective-permute-start | bytes 3145736 | tf_op jit(solution)/shard_map/ppermute | solution.py:15
  88.6 164.3 %all-gather.6.cloned.1.call-start = ((), (), s32[]{:S(2)}) async-start(), calls=%async_computation.1 | async-start | bytes 4718592 | tf_op jit(solution)/shard_map/all_gather | solution.py:29
  99.7 22.8 %collective-permute-start.5 = (bf16[2,256,1024]{2,1,0:T(8,128)(2,1)}, bf16[2,256,1024]{2,1,0:T(8,128)(2,1)}, u32[]{:S(2)}, u32[]{:S(2)}) collective-permute-start(bf16[2,256,1024]{2,1,0:T(8,128)(2,1)} %collective-permute-done.4), channel_id=1, source_target_pairs={{0,4},{4,8},{8,12},{12,16},{16,20},{20,24},{24,28},{28,32},{32,36}... | collective-permute-start | bytes 3145736 | tf_op jit(solution)/shard_map/ppermute | solution.py:15
  122.5 48.9 %collective-permute-start.6 = (bf16[2,256,1024]{2,1,0:T(8,128)(2,1)}, bf16[2,256,1024]{2,1,0:T(8,128)(2,1)}, u32[]{:S(2)}, u32[]{:S(2)}) collective-permute-start(bf16[2,256,1024]{2,1,0:T(8,128)(2,1)} %collective-permute-done.5), channel_id=1, source_target_pairs={{0,4},{4,8},{8,12},{12,16},{16,20},{20,24},{24,28},{28,32},{32,36}... | collective-permute-start | bytes 3145736 | tf_op jit(solution)/shard_map/ppermute | solution.py:15
  125.7 119.0 %copy-start.18 = (bf16[256,1024]{0,1:T(8,128)(2,1)}, bf16[256,1024]{0,1:T(8,128)(2,1)S(1)}, u32[]{:S(2)}) copy-start(bf16[256,1024]{0,1:T(8,128)(2,1)S(1)} %copy.22) | copy-start | bytes 1572868
  171.4 18.5 %collective-permute-start.7 = (bf16[2,256,1024]{2,1,0:T(8,128)(2,1)}, bf16[2,256,1024]{2,1,0:T(8,128)(2,1)}, u32[]{:S(2)}, u32[]{:S(2)}) collective-permute-start(bf16[2,256,1024]{2,1,0:T(8,128)(2,1)} %collective-permute-done.6), channel_id=1, source_target_pairs={{0,4},{4,8},{8,12},{12,16},{16,20},{20,24},{24,28},{28,32},{32,36}... | collective-permute-start | bytes 3145736 | tf_op jit(solution)/shard_map/ppermute | solution.py:15
  245.0 7.9 %copy-start.16 = (f32[8,128,128]{2,1,0:T(8,128)S(1)}, f32[8,128,128]{2,1,0:T(8,128)}, u32[]{:S(2)}) copy-start(f32[8,128,128]{2,1,0:T(8,128)} %slice_add_fusion.10) | copy-start | bytes 1572868
  245.0 7.9 %copy-start.17 = (f32[1,8,128,128]{3,2,1,0:T(8,128)S(1)}, f32[1,8,128,128]{3,2,1,0:T(8,128)}, u32[]{:S(2)}) copy-start(f32[1,8,128,128]{3,2,1,0:T(8,128)} %fusion.223) | copy-start | bytes 1572868
  252.9 8.4 %copy-start.19 = (bf16[256,1024]{0,1:T(8,128)(2,1)S(1)}, bf16[256,1024]{0,1:T(8,128)(2,1)}, u32[]{:S(2)}) copy-start(bf16[256,1024]{0,1:T(8,128)(2,1)} %copy-done.18) | copy-start | bytes 1572868
  252.9 9.0 %copy-start.15 = (f32[256,2304]{0,1:T(8,128)S(1)}, f32[256,2304]{0,1:T(8,128)}, u32[]{:S(2)}) copy-start(f32[256,2304]{0,1:T(8,128)} %copy-done.14) | copy-start | bytes 7077892
  262.0 7.7 %copy-start.9 = (f32[256,2304]{0,1:T(8,128)S(1)}, f32[256,2304]{0,1:T(8,128)}, u32[]{:S(2)}) copy-start(f32[256,2304]{0,1:T(8,128)} %copy-done.8) | copy-start | bytes 7077892
  264.9 7.5 %copy-start.7 = (f32[256,2304]{0,1:T(8,128)S(1)}, f32[256,2304]{0,1:T(8,128)}, u32[]{:S(2)}) copy-start(f32[256,2304]{0,1:T(8,128)} %copy-done.6) | copy-start | bytes 7077892
  267.3 7.3 %copy-start.5 = (f32[256,2304]{0,1:T(8,128)S(1)}, f32[256,2304]{0,1:T(8,128)}, u32[]{:S(2)}) copy-start(f32[256,2304]{0,1:T(8,128)} %copy-done.4) | copy-start | bytes 7077892
  269.7 7.4 %copy-start.3 = (f32[256,2304]{0,1:T(8,128)S(1)}, f32[256,2304]{0,1:T(8,128)}, u32[]{:S(2)}) copy-start(f32[256,2304]{0,1:T(8,128)} %copy-done.2) | copy-start | bytes 7077892
  269.7 11.7 %slice-start = ((s8[8388608]{0:T(1024)(128)(4,1)}), s8[4194304]{0:T(1024)(128)(4,1)S(1)}, s32[]{:S(2)}) async-start(s8[8388608]{0:T(1024)(128)(4,1)} %bitcast.235), calls=%async_computation.4 | async-start | bytes 8388608
  274.6 6.8 %slice-start.1 = ((s8[8388608]{0:T(1024)(128)(4,1)}), s8[4194304]{0:T(1024)(128)(4,1)S(1)}, s32[]{:S(2)}) async-start(s8[8388608]{0:T(1024)(128)(4,1)} %bitcast.235), calls=%async_computation.5 | async-start | bytes 8388608
  (21 other events, 47.5 us)
Sparse Core Ops, SparseCore 0:
  65.8 20.6 all-gather.7
  88.8 57.9 all-gather.9
  178.9 54.9 all-gather.5
where the time goes:
time: 322 us; the launch traced here: 320 us
  blocking collectives  82.3 us (26%)
  waiting for transfers between devices  80.5 us (25%)
  matrix products  56.5 us (18%)
  local copies, waits for them, and re-layouts  41.8 us (13%)
  other arithmetic  25 us (8%)
  between operations  19 us (6%)
  starting transfers between devices  15.4 us (5%)
    ppermute x8, waiting for transfers between devices, passed_along(): return lax.ppermute(block, axis, route)  77 us
    all_gather x3, blocking collectives, prefix_by_axis(): pieces = jax.tree.map(lambda part: lax.all_gather(part, axis), total)  53.7 us
    unnamed x113, local copies, waits for them, and re-layouts  38.1 us
    all_to_all x1, blocking collectives, summed_on_arrival(): lax.all_to_all(cut_along(value, dim, length), axis, 0, 0, tiled=True)  28.5 us
    dot_general x8, matrix products, body(): lax.dot_general(query_head, key_head, (((1,), (1,)), ((), ())), preferred...  24.5 us
    dot_general x8, matrix products, body(): jnp.dot(weights.astype(jnp.bfloat16), value_head, preferred_element_type=...  19.3 us
    ppermute x8, starting transfers between devices, passed_along(): return lax.ppermute(block, axis, route)  15.3 us
    dot_general x2, matrix products, memory_terms(): jnp.einsum('thd,the->hde', soft_keys, shaped_values, preferred_element_ty...  9.44 us
  transfers between devices with their start and end apart: 11, of which 7 were waited for; matrix products, arithmetic and copies ran while one was open for 24% of the time, Pallas kernels for 0%

commit v1 on v0

v1 whole, which is shorter than its diff:
```python
import jax
import jax.numpy as jnp
from jax import lax
from jax.experimental import pallas as pl
from jax.experimental.pallas import tpu as pltpu
from jax.sharding import Mesh
from jax.sharding import PartitionSpec as P

HD = 128
BLK = 256
NB = 8
PLANE = ("seq_1", "seq_2")
SCALE2 = (HD**-0.5) * 1.4426950408889634
F32 = jnp.float32
BF16 = jnp.bfloat16
ANY = pl.BlockSpec(memory_space=pl.ANY)
SMEM = pl.BlockSpec(memory_space=pltpu.SMEM)
VMEM = pl.BlockSpec(memory_space=pltpu.VMEM)


def shifted(block, axis, distance, wrap=True):
    size = lax.axis_size(axis)
    if wrap:
        route = [(i, (i + distance) % size) for i in range(size)]
    else:
        route = [(i, i + distance) for i in range(size - distance)]
    return lax.ppermute(block, axis, route)


def elu_plus(inputs):
    return jnp.where(inputs > 0, inputs + 1.0, jnp.exp(jnp.minimum(inputs, 0.0)))


def slot_of(here, d):
    return lax.rem(here - d + NB, NB)


def params(flops, nbytes):
    return dict(
        cost_estimate=pl.CostEstimate(flops=flops, bytes_accessed=nbytes, transcendentals=0),
        compiler_params=pltpu.CompilerParams(vmem_limit_bytes=48 * 1024 * 1024),
    )


def gather_pieces(here, pieces, buffer, sems, base, pick=None):
    copies = []
    for d, piece in enumerate(pieces):
        source = piece if pick is None else piece.at[pick]
        start = pl.multiple_of(slot_of(here, d) * BLK, BLK)
        copy = pltpu.make_async_copy(source, buffer.at[pl.ds(start, BLK)], sems.at[base + d])
        copy.start()
        copies.append(copy)
    return copies


def terms_kernel(*refs):
    pieces, out, kv, sems = refs[:NB], refs[NB], refs[NB + 1], refs[NB + 2]
    copies = []
    for d in range(NB):
        copy = pltpu.make_async_copy(pieces[d], kv.at[d], sems.at[d])
        copy.start()
        copies.append(copy)
    outer = jnp.zeros((HD, HD), F32)
    totals = jnp.zeros((8, HD), F32)
    for d in range(NB):
        copies[d].wait()
        soft = elu_plus(kv[d, 0].astype(F32)).astype(BF16)
        outer = outer + lax.dot_general(
            soft, kv[d, 1], (((0,), (0,)), ((), ())), preferred_element_type=F32
        )
        totals = totals + jnp.dot(jnp.ones((8, BLK), BF16), soft, preferred_element_type=F32)
    out[0:HD, :] = outer
    out[HD : HD + 8, :] = totals


def memory_terms(pieces):
    return pl.pallas_call(
        terms_kernel,
        out_shape=jax.ShapeDtypeStruct((HD + 8, HD), F32),
        in_specs=[ANY] * NB,
        out_specs=VMEM,
        scratch_shapes=[
            pltpu.VMEM((NB, 2, BLK, HD), BF16),
            pltpu.SemaphoreType.DMA((NB,)),
        ],
        name="terms",
        **params(2 * 2048 * HD * HD, 1 << 20),
    )(*pieces)


def attend(query, keys, values_ones, scores, first, count, mask_at, mask, start_max=None):
    peak = start_max
    for j in range(count):
        rows = pl.ds((first + j) * BLK, BLK)
        part = lax.dot_general(
            query, keys[rows, :], (((1,), (1,)), ((), ())), preferred_element_type=F32
        )
        if j == mask_at:
            part = jnp.where(mask, part, -jnp.inf)
        scores[:, j * BLK : (j + 1) * BLK] = part
        high = jnp.maximum(part[:, :HD], part[:, HD:])
        peak = high if peak is None else jnp.maximum(peak, high)
    peak = jnp.max(peak, axis=1, keepdims=True)
    shift = peak * SCALE2
    acc = None
    for j in range(count):
        rows = pl.ds((first + j) * BLK, BLK)
        weights = jnp.exp2(scores[:, j * BLK : (j + 1) * BLK] * SCALE2 - shift).astype(BF16)
        part = jnp.dot(weights, values_ones[rows, :], preferred_element_type=F32)
        acc = part if acc is None else acc + part
    return acc, peak


def own_kernel(*refs):
    here_ref = refs[0]
    kvs, qs = refs[1 : 1 + NB], refs[1 + NB : 1 + 2 * NB]
    acc_out, peak_out = refs[1 + 2 * NB : 3 + 2 * NB]
    keys, values, query, scores_a, scores_b, sems = refs[3 + 2 * NB :]
    here = here_ref[0]
    copies = gather_pieces(here, qs, query, sems, 0)
    copies += gather_pieces(here, kvs, keys, sems, NB, 0)
    copies += gather_pieces(here, kvs, values.at[:, pl.ds(0, HD)], sems, 2 * NB, 1)
    values[:, HD:] = jnp.ones((NB * BLK, HD), BF16)
    for copy in copies:
        copy.wait()
    row = lax.broadcasted_iota(jnp.int32, (BLK, BLK), 0)
    col = lax.broadcasted_iota(jnp.int32, (BLK, BLK), 1)
    for b in range(NB):
        rows = pl.ds(b * BLK, BLK)
        acc, peak = attend(
            query[rows, :], keys, values, (scores_a, scores_b)[b % 2], 0, b + 1, b, col <= row
        )
        acc_out[rows, :] = acc
        peak_out[rows, :] = jnp.broadcast_to(peak, (BLK, HD))


def own_part(here, kvs, qs):
    rows = NB * BLK
    return pl.pallas_call(
        own_kernel,
        out_shape=(
            jax.ShapeDtypeStruct((rows, 2 * HD), F32),
            jax.ShapeDtypeStruct((rows, HD), F32),
        ),
        in_specs=[SMEM] + [ANY] * (2 * NB),
        out_specs=(VMEM, VMEM),
        scratch_shapes=[
            pltpu.VMEM((rows, HD), BF16),
            pltpu.VMEM((rows, 2 * HD), BF16),
            pltpu.VMEM((rows, HD), BF16),
            pltpu.VMEM((BLK, rows), F32),
            pltpu.VMEM((BLK, rows), F32),
            pltpu.SemaphoreType.DMA((3 * NB,)),
        ],
        name="own",
        **params(36 * BLK * BLK * HD * 8, 5 << 20),
    )(here, *kvs, *qs)


def past_kernel(*refs):
    here_ref, beta_ref = refs[0], refs[1]
    kvs, qs = refs[2 : 2 + NB], refs[2 + NB : 2 + 2 * NB]
    acc_in, peak_in, memory_ref = refs[2 + 2 * NB : 5 + 2 * NB]
    outs = refs[5 + 2 * NB : 5 + 3 * NB]
    keys, values, query, scores_a, scores_b, result, acc_buf, sems = refs[5 + 3 * NB :]
    here, segment = here_ref[0], here_ref[1]
    copies = gather_pieces(here, qs, query, sems, 0)
    copies += gather_pieces(here, kvs, keys, sems, NB, 0)
    copies += gather_pieces(here, kvs, values.at[:, pl.ds(0, HD)], sems, 2 * NB, 1)
    values[:, HD:] = jnp.ones((NB * BLK, HD), BF16)
    for copy in copies:
        copy.wait()

    @pl.when(segment == 0)
    def _():
        acc_buf[...] = acc_in[...]

    @pl.when(segment > 0)
    def _():
        row = lax.broadcasted_iota(jnp.int32, (BLK, BLK), 0)
        col = lax.broadcasted_iota(jnp.int32, (BLK, BLK), 1)
        for b in range(NB):
            rows = pl.ds(b * BLK, BLK)
            before = peak_in[rows, :]
            acc, peak = attend(
                query[rows, :],
                keys,
                values,
                (scores_a, scores_b)[b % 2],
                b,
                NB - b,
                0,
                col > row,
                before,
            )
            fade = jnp.exp2((before - peak) * SCALE2)
            acc_buf[rows, :HD] = acc[:, :HD] + acc_in[rows, :HD] * fade
            acc_buf[rows, HD:] = acc[:, HD:] + acc_in[rows, HD:] * fade

    memory = memory_ref[0:HD, :]
    norm = jnp.transpose(jnp.broadcast_to(memory_ref[HD : HD + 1, :], (HD, HD)))
    whole = jnp.concatenate([memory, norm], axis=1)
    upper = whole.astype(BF16)
    lower = (whole - upper.astype(F32)).astype(BF16)
    split = jnp.concatenate([upper, lower], axis=0)
    gate = 1.0 / (1.0 + jnp.exp(-jnp.full((1, HD), beta_ref[here], F32)))
    for b in range(NB):
        rows = pl.ds(b * BLK, BLK)
        soft = elu_plus(query[rows, :].astype(F32)).astype(BF16)
        both = jnp.dot(jnp.concatenate([soft, soft], axis=1), split, preferred_element_type=F32)
        from_memory = both[:, :HD] / (1.0 + both[:, HD:])
        local = acc_buf[rows, :HD] / acc_buf[rows, HD:]
        result[rows, :] = (gate * from_memory + (1.0 - gate) * local).astype(BF16)
    leaving = []
    for d in range(NB):
        start = pl.multiple_of(slot_of(here, d) * BLK, BLK)
        copy = pltpu.make_async_copy(result.at[pl.ds(start, BLK)], outs[d], sems.at[d])
        copy.start()
        leaving.append(copy)
    for copy in leaving:
        copy.wait()


def past_part(here, beta, kvs, qs, acc, peak, memory):
    rows = NB * BLK
    return pl.pallas_call(
        past_kernel,
        out_shape=[jax.ShapeDtypeStruct((BLK, HD), BF16)] * NB,
        in_specs=[SMEM, SMEM] + [ANY] * (2 * NB) + [VMEM] * 3,
        out_specs=[ANY] * NB,
        scratch_shapes=[
            pltpu.VMEM((rows, HD), BF16),
            pltpu.VMEM((rows, 2 * HD), BF16),
            pltpu.VMEM((rows, HD), BF16),
            pltpu.VMEM((BLK, rows), F32),
            pltpu.VMEM((BLK, rows), F32),
            pltpu.VMEM((rows, HD), BF16),
            pltpu.VMEM((rows, 2 * HD), F32),
            pltpu.SemaphoreType.DMA((3 * NB,)),
        ],
        name="past",
        **params(36 * BLK * BLK * HD * 8, 6 << 20),
    )(here, beta, *kvs, *qs, acc, peak, memory)


def project_kernel(*refs):
    spot_ref = refs[0]
    pieces, weight = refs[1 : 1 + NB], refs[1 + NB]
    out = refs[2 + NB]
    attended, sems = refs[3 + NB :]

    @pl.when(pl.program_id(0) == 0)
    def _():
        copies = []
        for d in range(NB):
            start = pl.multiple_of(lax.rem(spot_ref[0] + d, NB) * HD, HD)
            copy = pltpu.make_async_copy(pieces[d], attended.at[:, pl.ds(start, HD)], sems.at[d])
            copy.start()
            copies.append(copy)
        for copy in copies:
            copy.wait()

    out[...] = jnp.dot(attended[...], weight[...], preferred_element_type=F32).astype(out.dtype)


def project(spot, pieces, weight, dtype):
    width = weight.shape[1] // 4
    steps = 4
    tile = width // steps
    grid_spec = pltpu.PrefetchScalarGridSpec(
        num_scalar_prefetch=1,
        grid=(steps,),
        in_specs=[ANY] * NB
        + [pl.BlockSpec((NB * HD, tile), lambda n, spot: (0, spot[1] * steps + n))],
        out_specs=pl.BlockSpec((BLK, tile), lambda n, spot: (0, n)),
        scratch_shapes=[
            pltpu.VMEM((BLK, NB * HD), BF16),
            pltpu.SemaphoreType.DMA((NB,)),
        ],
    )
    return pl.pallas_call(
        project_kernel,
        grid_spec=grid_spec,
        out_shape=jax.ShapeDtypeStruct((BLK, width), dtype),
        name="project",
        **params(2 * BLK * NB * HD * width, 3 << 20),
    )(spot, *pieces, weight)


def body(queries, keys, values, beta, w_out):
    here = lax.axis_index(PLANE)
    segment = lax.axis_index("seq_0")
    column = lax.axis_index("head")

    def cut(array, d):
        return lax.dynamic_slice_in_dim(array, ((here + d) % NB) * HD, HD, 1)

    kv_here = [
        jnp.stack((cut(keys, d), cut(values, d))) for d in range(NB)
    ]
    q_here = [cut(queries, d) for d in range(NB)]
    kvs = [kv_here[0]] + [shifted(kv_here[d], PLANE, d) for d in range(1, NB)]
    qs = [q_here[0]] + [shifted(q_here[d], PLANE, d) for d in range(1, NB)]
    kvs_past = [shifted(piece, "seq_0", 1, wrap=False) for piece in kvs]

    memory = shifted(memory_terms(kvs), "seq_0", 1, wrap=False)
    memory = memory + shifted(memory, "seq_0", 1, wrap=False)
    memory = memory + shifted(memory, "seq_0", 2, wrap=False)
    memory = memory + shifted(memory, "seq_0", 4, wrap=False)

    place = jnp.stack((here, segment)).astype(jnp.int32)
    acc, peak = own_part(place, kvs, qs)
    attended = past_part(place, beta, kvs_past, qs, acc, peak, memory)
    heads = [attended[0]] + [shifted(attended[d], PLANE, NB - d) for d in range(1, NB)]

    total = None
    for e in (2, 1, 3, 0):
        spot = jnp.stack((here, (column + e) % 4)).astype(jnp.int32)
        part = project(spot, heads, w_out, BF16 if e else F32)
        if e:
            part = shifted(part, "head", e).astype(F32)
        total = part if total is None else total + part
    return total.astype(BF16)


def solution(mesh):
    torus = Mesh(
        mesh.devices.reshape(8, 4, 2, mesh.shape["head"]), ("seq_0", "seq_1", "seq_2", "head")
    )
    seq = ("seq_0", "seq_1", "seq_2")
    return jax.shard_map(
        body,
        mesh=torus,
        in_specs=(P(seq, "head"), P(seq, "head"), P(seq, "head"), P("head"), P("head", None)),
        out_specs=P(seq, "head"),
        check_vma=False,
    )
```

time: 322 us -> 137 us (0.43)
  blocking collectives: 82.3 us -> 0 us
  matrix products: 56.5 us -> 0 us
  waiting for transfers between devices: 80.5 us -> 34.3 us
  starting transfers between devices: 15.4 us -> 61.4 us
  local copies, waits for them, and re-layouts: 41.8 us -> 2.49 us
  Pallas kernels: 0 us -> 33.4 us
  other arithmetic: 25 us -> 2.71 us
  between operations: 19 us -> 0.42 us
    dot_general x21 -> x0, matrix products: 56.5 us -> none  [the longest x8 24.5 us: body(): lax.dot_general(query_head, key_head, (((1,), (1,)), ((), ())), preferred...]
    all_gather x3 -> x0, blocking collectives: 53.7 us -> none  [prefix_by_axis(): pieces = jax.tree.map(lambda part: lax.all_gather(part, axis), total)]
    ppermute x8 -> x36, starting transfers between devices: 15.3 us -> 61.4 us  [shifted(): return lax.ppermute(block, axis, route)]
    ppermute x8 -> x36, waiting for transfers between devices: 77 us -> 34.3 us  [shifted(): return lax.ppermute(block, axis, route)]
    unnamed x113 -> x2, local copies, waits for them, and re-layouts: 38.1 us -> 0.01 us
    pallas_call x0 -> x7, Pallas kernels: none -> 33.4 us  [the longest x4 15.7 us: project(): pl.pallas_call(project_kernel, grid_spec=grid_spec, out_shape=jax.ShapeDt...]
    all_to_all x1 -> x0, blocking collectives: 28.5 us -> none  [summed_on_arrival(): lax.all_to_all(cut_along(value, dim, length), axis, 0, 0, tiled=True)]
    reduce_sum x11 -> x0, other arithmetic: 9.06 us -> none  [the longest x2 4.62 us: memory_terms(): totals = jnp.sum(soft_keys, axis=0, dtype=jnp.float32)]
  transfers between devices with their start and end apart: 11 -> 36, of which waited for: 7 -> 16; matrix products, arithmetic and copies ran while one was open for 24% -> 1% of each run, Pallas kernels for 0% -> 14%
where the time goes in v1:
time: 137 us; the launch traced here: 135 us
  starting transfers between devices  61.4 us (45%)
  waiting for transfers between devices  34.3 us (25%)
  Pallas kernels  33.4 us (24%)
  other arithmetic  2.71 us (2%)
  local copies, waits for them, and re-layouts  2.49 us (2%)
    ppermute x36, starting transfers between devices, shifted(): return lax.ppermute(block, axis, route)  61.4 us
    ppermute x36, waiting for transfers between devices, shifted(): return lax.ppermute(block, axis, route)  34.3 us
    pallas_call x4, Pallas kernels, project(): pl.pallas_call(project_kernel, grid_spec=grid_spec, out_shape=jax.ShapeDt...  15.7 us
    pallas_call x1, Pallas kernels, past_part(): pl.pallas_call(past_kernel, out_shape=[jax.ShapeDtypeStruct((BLK, HD), BF...  7.61 us
    pallas_call x1, Pallas kernels, own_part(): pl.pallas_call(own_kernel, out_shape=(jax.ShapeDtypeStruct((rows, 2 * HD)...  7.06 us
    pallas_call x1, Pallas kernels, memory_terms(): pl.pallas_call(terms_kernel, out_shape=jax.ShapeDtypeStruct((HD + 8, HD),...  3.02 us
  transfers between devices with their start and end apart: 36, of which 16 were waited for; matrix products, arithmetic and copies ran while one was open for 1% of the time, Pallas kernels for 14%

profile of v1, /device:TPU:64, one launch (start us, length us, event | category | flops | bytes accessed | tf_op | source)
XLA Modules:
  0.0 134.8 jit_solution(9643894501709875503)
XLA Ops:
  1.4 3.1 %collective-permute-start.11 = (bf16[2,256,128]{2,1,0:T(8,128)(2,1)S(1)}, bf16[2,256,128]{2,1,0:T(8,128)(2,1)S(1)}, u32[]{:S(2)}, u32[]{:S(2)}) collective-permute-start(bf16[2,256,128]{2,1,0:T(8,128)(2,1)S(1)} %pad_maximum_fusion.6), channel_id=1, source_target_pairs={{0,24},{4,28},{8,0},{12,4},{16,8},{20,12},{24,16},{28,20},{1,25},{... | collective-permute-start | bytes 393224 | tf_op jit(solution)/shard_map/ppermute | solution.py:27
  5.3 2.8 %collective-permute-start.9 = (bf16[2,256,128]{2,1,0:T(8,128)(2,1)S(1)}, bf16[2,256,128]{2,1,0:T(8,128)(2,1)S(1)}, u32[]{:S(2)}, u32[]{:S(2)}) collective-permute-start(bf16[2,256,128]{2,1,0:T(8,128)(2,1)S(1)} %pad_maximum_fusion.5), channel_id=1, source_target_pairs={{0,20},{4,24},{8,28},{12,0},{16,4},{20,8},{24,12},{28,16},{1,21},{... | collective-permute-start | bytes 393224 | tf_op jit(solution)/shard_map/ppermute | solution.py:27
  8.3 6.7 %collective-permute-done.13.refs_8_.refs_7_ = bf16[2,256,128]{2,1,0:T(8,128)(2,1)S(1)} collective-permute-done((bf16[2,256,128]{2,1,0:T(8,128)(2,1)S(1)}, bf16[2,256,128]{2,1,0:T(8,128)(2,1)S(1)}, u32[]{:S(2)}, u32[]{:S(2)}) %collective-permute-start.13) | collective-permute-done | bytes 131104 | tf_op jit(solution)/shard_map/ppermute | solution.py:27
  15.5 3.6 %collective-permute-done.3.refs_3_.refs_2_ = bf16[2,256,128]{2,1,0:T(8,128)(2,1)S(1)} collective-permute-done((bf16[2,256,128]{2,1,0:T(8,128)(2,1)S(1)}, bf16[2,256,128]{2,1,0:T(8,128)(2,1)S(1)}, u32[]{:S(2)}, u32[]{:S(2)}) %collective-permute-start.3) | collective-permute-done | bytes 131104 | tf_op jit(solution)/shard_map/ppermute | solution.py:27
  19.0 2.2 %collective-permute-done.1.refs_2_.refs_1_ = bf16[2,256,128]{2,1,0:T(8,128)(2,1)S(1)} collective-permute-done((bf16[2,256,128]{2,1,0:T(8,128)(2,1)S(1)}, bf16[2,256,128]{2,1,0:T(8,128)(2,1)S(1)}, u32[]{:S(2)}, u32[]{:S(2)}) %collective-permute-start.1) | collective-permute-done | bytes 131104 | tf_op jit(solution)/shard_map/ppermute | solution.py:27
  21.2 3.0 %terms.1 = f32[136,128]{1,0:T(8,128)S(1)} custom-call(bf16[2,256,128]{2,1,0:T(8,128)(2,1)S(1)} %pad_maximum_fusion.refs_1_.refs_0_, bf16[2,256,128]{2,1,0:T(8,128)(2,1)S(1)} %collective-permute-done.1.refs_2_.refs_1_, bf16[2,256,128]{2,1,0:T(8,128)(2,1)S(1)} %collective-permute-done.3.refs_3_.refs_2_, ...), custom_call_target="tpu_custom_call" | custom-call | flops 67108864 | bytes 1048576 | tf_op jit(solution)/shard_map/terms/pallas_call | solution.py:77
  24.3 3.8 %collective-permute-start.22 = (f32[136,128]{1,0:T(8,128)S(1)}, f32[136,128]{1,0:T(8,128)S(1)}, u32[]{:S(2)}, u32[]{:S(2)}) collective-permute-start(f32[136,128]{1,0:T(8,128)S(1)} %terms.1), channel_id=1, source_target_pairs={{0,32},{32,64},{64,96},{96,128},{128,160},{160,192},{192,224},{1,3... | collective-permute-start | bytes 208904 | tf_op jit(solution)/shard_map/ppermute | solution.py:27
  28.1 2.6 %collective-permute-done.22 = f32[136,128]{1,0:T(8,128)S(1)} collective-permute-done((f32[136,128]{1,0:T(8,128)S(1)}, f32[136,128]{1,0:T(8,128)S(1)}, u32[]{:S(2)}, u32[]{:S(2)}) %collective-permute-start.22) | collective-permute-done | bytes 69664 | tf_op jit(solution)/shard_map/ppermute | solution.py:27
  30.7 4.4 %collective-permute-start.23 = (f32[136,128]{1,0:T(8,128)S(1)}, f32[136,128]{1,0:T(8,128)S(1)}, u32[]{:S(2)}, u32[]{:S(2)}) collective-permute-start(f32[136,128]{1,0:T(8,128)S(1)} %collective-permute-done.22), channel_id=1, source_target_pairs={{0,32},{32,64},{64,96},{96,128},{128,160},{160,192},{192,224},{1,3... | collective-permute-start | bytes 208904 | tf_op jit(solution)/shard_map/ppermute | solution.py:27
  37.0 8.5 %collective-permute-start.24 = (f32[136,128]{1,0:T(8,128)S(1)}, f32[136,128]{1,0:T(8,128)S(1)}, u32[]{:S(2)}, u32[]{:S(2)}) collective-permute-start(f32[136,128]{1,0:T(8,128)S(1)} %add.184), channel_id=1, source_target_pairs={{0,64},{32,96},{64,128},{96,160},{128,192},{160,224},{1,65},{33,97... | collective-permute-start | bytes 208904 | tf_op jit(solution)/shard_map/ppermute | solution.py:27
  47.3 3.8 %collective-permute-start.18 = (bf16[256,128]{1,0:T(8,128)(2,1)S(1)}, bf16[256,128]{1,0:T(8,128)(2,1)S(1)}, u32[]{:S(2)}, u32[]{:S(2)}) collective-permute-start(bf16[256,128]{1,0:T(8,128)(2,1)S(1)} %get-tuple-element.27), channel_id=1, source_target_pairs={{0,16},{4,20},{8,24},{12,28},{16,0},{20,4},{24,8},{28,12},{1,17},{... | collective-permute-start | bytes 196616 | tf_op jit(solution)/shard_map/ppermute | solution.py:27
  55.5 2.5 %collective-permute-start.10 = (bf16[2,256,128]{2,1,0:T(8,128)(2,1)S(1)}, bf16[2,256,128]{2,1,0:T(8,128)(2,1)S(1)}, u32[]{:S(2)}, u32[]{:S(2)}) collective-permute-start(bf16[2,256,128]{2,1,0:T(8,128)(2,1)S(1)} %collective-permute-done.9.refs_6_.refs_5_), channel_id=1, source_target_pairs={{0,32},{32,64},{64,96},{96,128},{128,160},{160,192},{192,224},{1,3... | collective-permute-start | bytes 393224 | tf_op jit(solution)/shard_map/ppermute | solution.py:27
  58.0 2.7 %collective-permute-start.12 = (bf16[2,256,128]{2,1,0:T(8,128)(2,1)S(1)}, bf16[2,256,128]{2,1,0:T(8,128)(2,1)S(1)}, u32[]{:S(2)}, u32[]{:S(2)}) collective-permute-start(bf16[2,256,128]{2,1,0:T(8,128)(2,1)S(1)} %collective-permute-done.11.refs_7_.refs_6_), channel_id=1, source_target_pairs={{0,32},{32,64},{64,96},{96,128},{128,160},{160,192},{192,224},{1,3... | collective-permute-start | bytes 393224 | tf_op jit(solution)/shard_map/ppermute | solution.py:27
  64.7 2.5 %collective-permute-start.8 = (bf16[2,256,128]{2,1,0:T(8,128)(2,1)S(1)}, bf16[2,256,128]{2,1,0:T(8,128)(2,1)S(1)}, u32[]{:S(2)}, u32[]{:S(2)}) collective-permute-start(bf16[2,256,128]{2,1,0:T(8,128)(2,1)S(1)} %collective-permute-done.7.refs_5_.refs_4_), channel_id=1, source_target_pairs={{0,32},{32,64},{64,96},{96,128},{128,160},{160,192},{192,224},{1,3... | collective-permute-start | bytes 393224 | tf_op jit(solution)/shard_map/ppermute | solution.py:27
  73.3 7.1 %own.1 = (f32[2048,256]{1,0:T(8,128)S(1)}, f32[2048,128]{1,0:T(8,128)S(1)}) custom-call(s32[2]{0:T(128)S(1)} %pad_add_fusion.1.refs_0_, bf16[2,256,128]{2,1,0:T(8,128)(2,1)S(1)} %pad_maximum_fusion.refs_1_.refs_0_, bf16[2,256,128]{2,1,0:T(8,128)(2,1)S(1)} %collective-permute-done.1.refs_2_.refs_1_, ...), custom_call_target="tpu_custom_call" | custom-call | flops 2415919104 | bytes 5242880 | tf_op jit(solution)/shard_map/own/pallas_call | solution.py:139
  82.5 7.6 %past.1 = (bf16[256,128]{1,0:T(8,128)(2,1)S(1)}, bf16[256,128]{1,0:T(8,128)(2,1)S(1)}, bf16[256,128]{1,0:T(8,128)(2,1)S(1)}, bf16[256,128]{1,0:T(8,128)(2,1)S(1)...) custom-call(s32[2]{0:T(128)S(1)} %pad_add_fusion.1.refs_0_, ...), custom_call_target="tpu_custom_call" | custom-call | flops 2415919104 | bytes 6291456 | tf_op jit(solution)/shard_map/past/pallas_call | solution.py:226
  102.7 3.9 %project.4 = bf16[256,1024]{1,0:T(8,128)(2,1)S(1)} custom-call(s32[2]{0:T(128)S(1)} %pad_add_fusion.refs_0_, bf16[256,128]{1,0:T(8,128)(2,1)S(1)} %get-tuple-element.17.refs_1_, bf16[256,128]{1,0:T(8,128)(2,1)S(1)} %collective-permute-done.26.refs_2_, bf16[256,128]{1,0:T(8,128)(2,1)S(1)} %collective-permute-done.27.refs_3_, ...), custom_call_target="tpu_custom_call" | custom-call | flops 536870912 | bytes 3145728 | tf_op jit(solution)/shard_map/project/pallas_call | solution.py:281
  106.6 3.1 %collective-permute-start.33 = (bf16[256,1024]{1,0:T(8,128)(2,1)S(1)}, bf16[256,1024]{1,0:T(8,128)(2,1)S(1)}, u32[]{:S(2)}, u32[]{:S(2)}) collective-permute-start(bf16[256,1024]{1,0:T(8,128)(2,1)S(1)} %project.4), channel_id=1, source_target_pairs={{0,2},{1,3},{2,0},{3,1},{4,6},{5,7},{6,4},{7,5},{8,10},{9,11},{10,... | collective-permute-start | bytes 1572872 | tf_op jit(solution)/shard_map/ppermute | solution.py:27
  109.8 3.9 %project.5 = bf16[256,1024]{1,0:T(8,128)(2,1)S(1)} custom-call(s32[2]{0:T(128)S(1)} %pad_add_fusion.2.refs_0_, bf16[256,128]{1,0:T(8,128)(2,1)S(1)} %get-tuple-element.17.refs_1_, bf16[256,128]{1,0:T(8,128)(2,1)S(1)} %collective-permute-done.26.refs_2_, bf16[256,128]{1,0:T(8,128)(2,1)S(1)} %collective-permute-done.27.refs_3_, ...), custom_call_target="tpu_custom_call" | custom-call | flops 536870912 | bytes 3145728 | tf_op jit(solution)/shard_map/project/pallas_call | solution.py:281
  114.4 3.9 %project.6 = bf16[256,1024]{1,0:T(8,128)(2,1)S(1)} custom-call(s32[2]{0:T(128)S(1)} %pad_add_fusion.3.refs_0_, bf16[256,128]{1,0:T(8,128)(2,1)S(1)} %get-tuple-element.17.refs_1_, bf16[256,128]{1,0:T(8,128)(2,1)S(1)} %collective-permute-done.26.refs_2_, bf16[256,128]{1,0:T(8,128)(2,1)S(1)} %collective-permute-done.27.refs_3_, ...), custom_call_target="tpu_custom_call" | custom-call | flops 536870912 | bytes 3145728 | tf_op jit(solution)/shard_map/project/pallas_call | solution.py:281
  118.3 2.7 %collective-permute-start.35 = (bf16[256,1024]{1,0:T(8,128)(2,1)S(1)}, bf16[256,1024]{1,0:T(8,128)(2,1)}, u32[]{:S(2)}, u32[]{:S(2)}) collective-permute-start(bf16[256,1024]{1,0:T(8,128)(2,1)S(1)} %project.6), channel_id=1, source_target_pairs={{0,3},{1,0},{2,1},{3,2},{4,7},{5,4},{6,5},{7,6},{8,11},{9,8},{10,9... | collective-permute-start | bytes 1572872 | tf_op jit(solution)/shard_map/ppermute | solution.py:27
  121.1 3.9 %project.7 = f32[256,1024]{1,0:T(8,128)S(1)} custom-call(s32[2]{0:T(128)S(1)} %pad_add_fusion.4.refs_0_, bf16[256,128]{1,0:T(8,128)(2,1)S(1)} %get-tuple-element.17.refs_1_, bf16[256,128]{1,0:T(8,128)(2,1)S(1)} %collective-permute-done.26.refs_2_, bf16[256,128]{1,0:T(8,128)(2,1)S(1)} %collective-permute-done.27.refs_3_, ...), custom_call_target="tpu_custom_call" | custom-call | flops 536870912 | bytes 3145728 | tf_op jit(solution)/shard_map/project/pallas_call | solution.py:281
  125.0 7.4 %collective-permute-done.34 = bf16[256,1024]{1,0:T(8,128)(2,1)S(1)} collective-permute-done((bf16[256,1024]{1,0:T(8,128)(2,1)S(1)}, bf16[256,1024]{1,0:T(8,128)(2,1)S(1)}, u32[]{:S(2)}, u32[]{:S(2)}) %collective-permute-start.34) | collective-permute-done | bytes 524320 | tf_op jit(solution)/shard_map/ppermute | solution.py:27
  132.6 2.2 %add_convert_fusion = bf16[256,1024]{1,0:T(8,128)(2,1)} fusion(f32[256,1024]{1,0:T(8,128)S(1)} %project.7, bf16[256,1024]{1,0:T(8,128)(2,1)} %collective-permute-done.35, bf16[256,1024]{1,0:T(8,128)(2,1)S(1)} %collective-permute-done.34, bf16[256,1024]{1,0:T(8,128)(2,1)S(1)} %collective-permute-done.33), kind=kLoop, calls=%fused_computation | loop fusion | flops 1835008 | bytes 3145728 | tf_op jit(solution)/shard_map/convert_element_type | solution.py:323
  (76 shorter events, 36.5 us)
Async XLA Ops:
  1.4 6.8 %collective-permute-start.11 = (bf16[2,256,128]{2,1,0:T(8,128)(2,1)S(1)}, bf16[2,256,128]{2,1,0:T(8,128)(2,1)S(1)}, u32[]{:S(2)}, u32[]{:S(2)}) collective-permute-start(bf16[2,256,128]{2,1,0:T(8,128)(2,1)S(1)} %pad_maximum_fusion.6), channel_id=1, source_target_pairs={{0,24},{4,28},{8,0},{12,4},{16,8},{20,12},{24,16},{28,20},{1,25},{... | collective-permute-start | bytes 393224 | tf_op jit(solution)/shard_map/ppermute | solution.py:27
  4.5 10.5 %collective-permute-start.13 = (bf16[2,256,128]{2,1,0:T(8,128)(2,1)S(1)}, bf16[2,256,128]{2,1,0:T(8,128)(2,1)S(1)}, u32[]{:S(2)}, u32[]{:S(2)}) collective-permute-start(bf16[2,256,128]{2,1,0:T(8,128)(2,1)S(1)} %pad_maximum_fusion.7), channel_id=1, source_target_pairs={{0,28},{4,0},{8,4},{12,8},{16,12},{20,16},{24,20},{28,24},{1,29},{... | collective-permute-start | bytes 393224 | tf_op jit(solution)/shard_map/ppermute | solution.py:27
  4.5 10.5 %collective-permute-start.7 = (bf16[2,256,128]{2,1,0:T(8,128)(2,1)S(1)}, bf16[2,256,128]{2,1,0:T(8,128)(2,1)S(1)}, u32[]{:S(2)}, u32[]{:S(2)}) collective-permute-start(bf16[2,256,128]{2,1,0:T(8,128)(2,1)S(1)} %pad_maximum_fusion.4), channel_id=1, source_target_pairs={{0,16},{4,20},{8,24},{12,28},{16,0},{20,4},{24,8},{28,12},{1,17},{... | collective-permute-start | bytes 393224 | tf_op jit(solution)/shard_map/ppermute | solution.py:27
  5.3 9.8 %collective-permute-start.9 = (bf16[2,256,128]{2,1,0:T(8,128)(2,1)S(1)}, bf16[2,256,128]{2,1,0:T(8,128)(2,1)S(1)}, u32[]{:S(2)}, u32[]{:S(2)}) collective-permute-start(bf16[2,256,128]{2,1,0:T(8,128)(2,1)S(1)} %pad_maximum_fusion.5), channel_id=1, source_target_pairs={{0,20},{4,24},{8,28},{12,0},{16,4},{20,8},{24,12},{28,16},{1,21},{... | collective-permute-start | bytes 393224 | tf_op jit(solution)/shard_map/ppermute | solution.py:27
  8.1 7.4 %collective-permute-start.5 = (bf16[2,256,128]{2,1,0:T(8,128)(2,1)S(1)}, bf16[2,256,128]{2,1,0:T(8,128)(2,1)S(1)}, u32[]{:S(2)}, u32[]{:S(2)}) collective-permute-start(bf16[2,256,128]{2,1,0:T(8,128)(2,1)S(1)} %pad_maximum_fusion.3), channel_id=1, source_target_pairs={{0,12},{4,16},{8,20},{12,24},{16,28},{20,0},{24,4},{28,8},{1,13},{... | collective-permute-start | bytes 393224 | tf_op jit(solution)/shard_map/ppermute | solution.py:27
  8.2 10.8 %collective-permute-start.3 = (bf16[2,256,128]{2,1,0:T(8,128)(2,1)S(1)}, bf16[2,256,128]{2,1,0:T(8,128)(2,1)S(1)}, u32[]{:S(2)}, u32[]{:S(2)}) collective-permute-start(bf16[2,256,128]{2,1,0:T(8,128)(2,1)S(1)} %pad_maximum_fusion.2), channel_id=1, source_target_pairs={{0,8},{4,12},{8,16},{12,20},{16,24},{20,28},{24,0},{28,4},{1,9},{5... | collective-permute-start | bytes 393224 | tf_op jit(solution)/shard_map/ppermute | solution.py:27
  37.0 21.0 %collective-permute-start.24 = (f32[136,128]{1,0:T(8,128)S(1)}, f32[136,128]{1,0:T(8,128)S(1)}, u32[]{:S(2)}, u32[]{:S(2)}) collective-permute-start(f32[136,128]{1,0:T(8,128)S(1)} %add.184), channel_id=1, source_target_pairs={{0,64},{32,96},{64,128},{96,160},{128,192},{160,224},{1,65},{33,97... | collective-permute-start | bytes 208904 | tf_op jit(solution)/shard_map/ppermute | solution.py:27
  46.7 6.8 %collective-permute-start.16 = (bf16[256,128]{1,0:T(8,128)(2,1)S(1)}, bf16[256,128]{1,0:T(8,128)(2,1)S(1)}, u32[]{:S(2)}, u32[]{:S(2)}) collective-permute-start(bf16[256,128]{1,0:T(8,128)(2,1)S(1)} %get-tuple-element.29), channel_id=1, source_target_pairs={{0,8},{4,12},{8,16},{12,20},{16,24},{20,28},{24,0},{28,4},{1,9},{5... | collective-permute-start | bytes 196616 | tf_op jit(solution)/shard_map/ppermute | solution.py:27
  46.7 7.6 %collective-permute-start.17 = (bf16[256,128]{1,0:T(8,128)(2,1)S(1)}, bf16[256,128]{1,0:T(8,128)(2,1)S(1)}, u32[]{:S(2)}, u32[]{:S(2)}) collective-permute-start(bf16[256,128]{1,0:T(8,128)(2,1)S(1)} %get-tuple-element.28), channel_id=1, source_target_pairs={{0,12},{4,16},{8,20},{12,24},{16,28},{20,0},{24,4},{28,8},{1,13},{... | collective-permute-start | bytes 196616 | tf_op jit(solution)/shard_map/ppermute | solution.py:27
  47.3 8.2 %collective-permute-start.18 = (bf16[256,128]{1,0:T(8,128)(2,1)S(1)}, bf16[256,128]{1,0:T(8,128)(2,1)S(1)}, u32[]{:S(2)}, u32[]{:S(2)}) collective-permute-start(bf16[256,128]{1,0:T(8,128)(2,1)S(1)} %get-tuple-element.27), channel_id=1, source_target_pairs={{0,16},{4,20},{8,24},{12,28},{16,0},{20,4},{24,8},{28,12},{1,17},{... | collective-permute-start | bytes 196616 | tf_op jit(solution)/shard_map/ppermute | solution.py:27
  51.6 13.1 %collective-permute-start = (bf16[2,256,128]{2,1,0:T(8,128)(2,1)S(1)}, bf16[2,256,128]{2,1,0:T(8,128)(2,1)S(1)}, u32[]{:S(2)}, u32[]{:S(2)}) collective-permute-start(bf16[2,256,128]{2,1,0:T(8,128)(2,1)S(1)} %pad_maximum_fusion.refs_1_.refs_0_), channel_id=1, source_target_pairs={{0,32},{32,64},{64,96},{96,128},{128,160},{160,192},{192,224},{1,3... | collective-permute-start | bytes 393224 | tf_op jit(solution)/shard_map/ppermute | solution.py:27
  53.5 7.3 %collective-permute-start.19 = (bf16[256,128]{1,0:T(8,128)(2,1)S(1)}, bf16[256,128]{1,0:T(8,128)(2,1)S(1)}, u32[]{:S(2)}, u32[]{:S(2)}) collective-permute-start(bf16[256,128]{1,0:T(8,128)(2,1)S(1)} %get-tuple-element.26), channel_id=1, source_target_pairs={{0,20},{4,24},{8,28},{12,0},{16,4},{20,8},{24,12},{28,16},{1,21},{... | collective-permute-start | bytes 196616 | tf_op jit(solution)/shard_map/ppermute | solution.py:27
  55.5 11.7 %collective-permute-start.10 = (bf16[2,256,128]{2,1,0:T(8,128)(2,1)S(1)}, bf16[2,256,128]{2,1,0:T(8,128)(2,1)S(1)}, u32[]{:S(2)}, u32[]{:S(2)}) collective-permute-start(bf16[2,256,128]{2,1,0:T(8,128)(2,1)S(1)} %collective-permute-done.9.refs_6_.refs_5_), channel_id=1, source_target_pairs={{0,32},{32,64},{64,96},{96,128},{128,160},{160,192},{192,224},{1,3... | collective-permute-start | bytes 393224 | tf_op jit(solution)/shard_map/ppermute | solution.py:27
  58.0 11.3 %collective-permute-start.12 = (bf16[2,256,128]{2,1,0:T(8,128)(2,1)S(1)}, bf16[2,256,128]{2,1,0:T(8,128)(2,1)S(1)}, u32[]{:S(2)}, u32[]{:S(2)}) collective-permute-start(bf16[2,256,128]{2,1,0:T(8,128)(2,1)S(1)} %collective-permute-done.11.refs_7_.refs_6_), channel_id=1, source_target_pairs={{0,32},{32,64},{64,96},{96,128},{128,160},{160,192},{192,224},{1,3... | collective-permute-start | bytes 393224 | tf_op jit(solution)/shard_map/ppermute | solution.py:27
  60.8 10.4 %collective-permute-start.25 = (f32[136,128]{1,0:T(8,128)S(1)}, f32[136,128]{1,0:T(8,128)S(1)}, u32[]{:S(2)}, u32[]{:S(2)}) collective-permute-start(f32[136,128]{1,0:T(8,128)S(1)} %add.185), channel_id=1, source_target_pairs={{0,128},{32,160},{64,192},{96,224},{1,129},{33,161},{65,193},{97,2... | collective-permute-start | bytes 208904 | tf_op jit(solution)/shard_map/ppermute | solution.py:27
  62.7 17.7 %collective-permute-start.14 = (bf16[2,256,128]{2,1,0:T(8,128)(2,1)S(1)}, bf16[2,256,128]{2,1,0:T(8,128)(2,1)S(1)}, u32[]{:S(2)}, u32[]{:S(2)}) collective-permute-start(bf16[2,256,128]{2,1,0:T(8,128)(2,1)S(1)} %collective-permute-done.13.refs_8_.refs_7_), channel_id=1, source_target_pairs={{0,32},{32,64},{64,96},{96,128},{128,160},{160,192},{192,224},{1,3... | collective-permute-start | bytes 393224 | tf_op jit(solution)/shard_map/ppermute | solution.py:27
  64.7 15.7 %collective-permute-start.8 = (bf16[2,256,128]{2,1,0:T(8,128)(2,1)S(1)}, bf16[2,256,128]{2,1,0:T(8,128)(2,1)S(1)}, u32[]{:S(2)}, u32[]{:S(2)}) collective-permute-start(bf16[2,256,128]{2,1,0:T(8,128)(2,1)S(1)} %collective-permute-done.7.refs_5_.refs_4_), channel_id=1, source_target_pairs={{0,32},{32,64},{64,96},{96,128},{128,160},{160,192},{192,224},{1,3... | collective-permute-start | bytes 393224 | tf_op jit(solution)/shard_map/ppermute | solution.py:27
  67.3 13.2 %collective-permute-start.6 = (bf16[2,256,128]{2,1,0:T(8,128)(2,1)S(1)}, bf16[2,256,128]{2,1,0:T(8,128)(2,1)S(1)}, u32[]{:S(2)}, u32[]{:S(2)}) collective-permute-start(bf16[2,256,128]{2,1,0:T(8,128)(2,1)S(1)} %collective-permute-done.5.refs_4_.refs_3_), channel_id=1, source_target_pairs={{0,32},{32,64},{64,96},{96,128},{128,160},{160,192},{192,224},{1,3... | collective-permute-start | bytes 393224 | tf_op jit(solution)/shard_map/ppermute | solution.py:27
  69.3 11.2 %collective-permute-start.4 = (bf16[2,256,128]{2,1,0:T(8,128)(2,1)S(1)}, bf16[2,256,128]{2,1,0:T(8,128)(2,1)S(1)}, u32[]{:S(2)}, u32[]{:S(2)}) collective-permute-start(bf16[2,256,128]{2,1,0:T(8,128)(2,1)S(1)} %collective-permute-done.3.refs_3_.refs_2_), channel_id=1, source_target_pairs={{0,32},{32,64},{64,96},{96,128},{128,160},{160,192},{192,224},{1,3... | collective-permute-start | bytes 393224 | tf_op jit(solution)/shard_map/ppermute | solution.py:27
  71.2 11.3 %collective-permute-start.2 = (bf16[2,256,128]{2,1,0:T(8,128)(2,1)S(1)}, bf16[2,256,128]{2,1,0:T(8,128)(2,1)S(1)}, u32[]{:S(2)}, u32[]{:S(2)}) collective-permute-start(bf16[2,256,128]{2,1,0:T(8,128)(2,1)S(1)} %collective-permute-done.1.refs_2_.refs_1_), channel_id=1, source_target_pairs={{0,32},{32,64},{64,96},{96,128},{128,160},{160,192},{192,224},{1,3... | collective-permute-start | bytes 393224 | tf_op jit(solution)/shard_map/ppermute | solution.py:27
  94.9 7.4 %collective-permute-start.31 = (bf16[256,128]{1,0:T(8,128)(2,1)S(1)}, bf16[256,128]{1,0:T(8,128)(2,1)S(1)}, u32[]{:S(2)}, u32[]{:S(2)}) collective-permute-start(bf16[256,128]{1,0:T(8,128)(2,1)S(1)} %get-tuple-element.23), channel_id=1, source_target_pairs={{0,8},{4,12},{8,16},{12,20},{16,24},{20,28},{24,0},{28,4},{1,9},{5... | collective-permute-start | bytes 196616 | tf_op jit(solution)/shard_map/ppermute | solution.py:27
  106.6 18.4 %collective-permute-start.33 = (bf16[256,1024]{1,0:T(8,128)(2,1)S(1)}, bf16[256,1024]{1,0:T(8,128)(2,1)S(1)}, u32[]{:S(2)}, u32[]{:S(2)}) collective-permute-start(bf16[256,1024]{1,0:T(8,128)(2,1)S(1)} %project.4), channel_id=1, source_target_pairs={{0,2},{1,3},{2,0},{3,1},{4,6},{5,7},{6,4},{7,5},{8,10},{9,11},{10,... | collective-permute-start | bytes 1572872 | tf_op jit(solution)/shard_map/ppermute | solution.py:27
  113.7 18.7 %collective-permute-start.34 = (bf16[256,1024]{1,0:T(8,128)(2,1)S(1)}, bf16[256,1024]{1,0:T(8,128)(2,1)S(1)}, u32[]{:S(2)}, u32[]{:S(2)}) collective-permute-start(bf16[256,1024]{1,0:T(8,128)(2,1)S(1)} %project.5), channel_id=1, source_target_pairs={{0,1},{1,2},{2,3},{3,0},{4,5},{5,6},{6,7},{7,4},{8,9},{9,10},{10,1... | collective-permute-start | bytes 1572872 | tf_op jit(solution)/shard_map/ppermute | solution.py:27
  118.3 14.3 %collective-permute-start.35 = (bf16[256,1024]{1,0:T(8,128)(2,1)S(1)}, bf16[256,1024]{1,0:T(8,128)(2,1)}, u32[]{:S(2)}, u32[]{:S(2)}) collective-permute-start(bf16[256,1024]{1,0:T(8,128)(2,1)S(1)} %project.6), channel_id=1, source_target_pairs={{0,3},{1,0},{2,1},{3,2},{4,7},{5,4},{6,5},{7,6},{8,11},{9,8},{10,9... | collective-permute-start | bytes 1572872 | tf_op jit(solution)/shard_map/ppermute | solution.py:27
  (13 other events, 148.6 us)
